TPU v7x, 32 devices: a whole 2x2x4 slice. The times are simulated.
32 devices in a mesh: span: 32 (over z, y, x, core).
Axes of the slice: x: 2, y: 2, z: 4, core: 2. Of those that a mesh axis runs over, the one named last changes fastest.
Arguments:
- random_slabs: bfloat16 [1024, 4, 3, 2048], P('span'), may hold values from -6 to 6
- span_weights: float32 [513], replicated, may hold values from 0.1 to 2
- wall_filter: bfloat16 [2048, 2048], replicated, may hold values from -0.125 to 0.125
- prev_state: float32 [1024, 3, 2048], P('span'), may hold values from -6 to 6
- time_scale: float32 [3, 2048], replicated, may hold values from 1 to 32
- mean_velocity: float32 [2048], replicated, may hold values from 0 to 2
- lund_diag: float32 [3, 2048], replicated, may hold values from 0.3 to 3
- lund_off: float32 [3, 2048], replicated, may hold values from -1 to 1
Outputs:
- velocity: bfloat16 [1024, 4, 3, 2048], P('span')
- new_state: float32 [1024, 3, 2048], P('span')
All inputs are finite; a program needn't handle non-finite values.
Results may differ from a plain program's by a relative error of at most 0.0051.
Values may be sent and summed in bfloat16 or wider, within the bound.
A program may use at most 128 MiB of HBM per device.

v0:
```python
import jax
import jax.numpy as jnp
from jax import lax
from jax.sharding import PartitionSpec as P


def from_partner(value, axis, bit):
    return lax.ppermute(value, axis, [(i, i ^ 1 << bit) for i in range(lax.axis_size(axis))])


def band_matrix(taps, height):
    reach = taps.shape[0]
    padded = jnp.concatenate([taps, jnp.zeros((height,), taps.dtype)])
    length = reach + height
    tiled = jnp.tile(padded, height)[: height * (length - 1)]
    return tiled.reshape(height, length - 1)


def butterfly(held, forward):
    count = lax.axis_size("span")
    device = lax.axis_index("span")
    levels = count.bit_length() - 1
    for level in range(levels - 1, -1, -1):
        groups, inner_first, targets, inner_last = held.shape
        halves = held.reshape(groups, inner_first, 2, targets // 2, inner_last)
        lower = halves[:, :, 0]
        higher = halves[:, :, 1]
        upper = device >> level & 1 == 1
        kept = jnp.where(upper, higher, lower)
        given = jnp.where(upper, lower, higher)
        if forward:
            taken = from_partner(given, "span", level)
        else:
            taken = from_partner(given, "span", level)
        first = jnp.where(upper, taken, kept)
        second = jnp.where(upper, kept, taken)
        held = jnp.stack([first, second], axis=1).reshape(
            groups * 2, inner_first, targets // 2, inner_last
        )
    return held


def body(
    random_slabs,
    span_weights,
    wall_filter,
    prev_state,
    time_scale,
    mean_velocity,
    lund_diag,
    lund_off,
):
    rows = random_slabs.shape[0]
    planes = random_slabs.shape[1]
    width = random_slabs.shape[3]
    columns = planes * 3 * width
    flat = random_slabs.reshape(rows, columns)
    scaling = jnp.sqrt(jnp.sum(span_weights * span_weights))
    taps = (span_weights / scaling).astype(jnp.bfloat16)
    reach = (span_weights.shape[0] - 1) // 2
    count = lax.axis_size("span")
    slim = columns // count
    held = butterfly(flat.reshape(1, rows, count, slim), True)
    total = rows * count
    whole = held.reshape(total, slim)
    height = min(512, total)
    matrix = band_matrix(taps, height)
    wrapped = jnp.concatenate([whole[total - reach :], whole, whole[:reach]], axis=0)

    def one_block(start):
        window = lax.dynamic_slice_in_dim(wrapped, start, height + 2 * reach, 0)
        return jnp.dot(matrix, window, preferred_element_type=jnp.float32)

    starts = jnp.arange(total // height) * height
    summed_cols = lax.map(one_block, starts).reshape(total, slim)
    rounded = summed_cols.astype(jnp.bfloat16)
    returned = butterfly(rounded.reshape(1, 1, count, rows * slim), False)
    spanned = returned.reshape(count, rows, slim).transpose(1, 0, 2).reshape(rows, planes, 3, width)
    filtered = lax.dot_general(
        spanned, wall_filter, (((3,), (1,)), ((), ())), preferred_element_type=jnp.float32
    )
    decay = jnp.exp(-jnp.pi / (2.0 * time_scale))
    inject = jnp.sqrt(1.0 - jnp.exp(-jnp.pi / time_scale))
    state = prev_state
    outputs = []
    for plane in range(planes):
        state = decay * state + inject * filtered[:, plane]
        along = state[:, 0]
        normal = state[:, 1]
        spanwise = state[:, 2]
        first = mean_velocity + lund_diag[0] * along
        second = lund_off[0] * along + lund_diag[1] * normal
        third = lund_off[1] * along + lund_off[2] * normal + lund_diag[2] * spanwise
        outputs.append(jnp.stack([first, second, third], axis=1).astype(jnp.bfloat16))
    velocity = jnp.stack(outputs, axis=1)
    return (velocity, state)


def solution(mesh):
    placed = (P("span", None, None, None), P(), P(), P("span", None, None), P(), P(), P(), P())
    return jax.shard_map(
        body,
        mesh=mesh,
        in_specs=placed,
        out_specs=(P("span", None, None, None), P("span", None, None)),
        check_vma=False,
    )
```

profile of v0, /device:TPU:0, one launch (start us, length us, event | category | flops | bytes accessed | tf_op | source)
XLA Modules:
  0.0 253.5 jit_solution(12371556991977251959)
XLA Ops:
  0.6 4.2 %copy.148 = bf16[32,4,3,2048]{3,2,1,0:T(4,128)(2,1)} copy(bf16[32,4,3,2048]{3,1,2,0:T(4,128)(2,1)} %param.10) | data formatting | bytes 3145728 | tf_op args[0]
  4.9 4.2 %reshape_reshape_reshape.3 = bf16[1,32,2,16,768]{4,3,2,1,0:T(8,128)(2,1)S(1)} reshape(bf16[32,4,3,2048]{3,2,1,0:T(4,128)(2,1)} %copy.148) | data formatting | bytes 3145728 | tf_op jit(solution)/shard_map/reshape;reshape;reshape | solution.py:25
  9.2 4.1 %collective-permute-start = (bf16[1,32,16,768]{3,2,1,0:T(8,128)(2,1)S(1)}, bf16[1,32,16,768]{3,2,1,0:T(8,128)(2,1)S(1)}, u32[]{:S(2)}, u32[]{:S(2)}) collective-permute-start(bf16[1,32,16,768]{3,2,1,0:T(8,128)(2,1)S(1)} %fusion.28), channel_id=1, source_target_pairs={{0,16},{1,17},{2,18},{3,19},{4,20},{5,21},{6,22},{7,23},{8,24},{9,... | collective-permute-start | bytes 2359304 | tf_op jit(solution)/shard_map/ppermute | solution.py:8
  13.3 34.4 %collective-permute-done = bf16[1,32,16,768]{3,2,1,0:T(8,128)(2,1)S(1)} collective-permute-done((bf16[1,32,16,768]{3,2,1,0:T(8,128)(2,1)S(1)}, bf16[1,32,16,768]{3,2,1,0:T(8,128)(2,1)S(1)}, u32[]{:S(2)}, u32[]{:S(2)}) %collective-permute-start) | collective-permute-done | bytes 786464 | tf_op jit(solution)/shard_map/ppermute | solution.py:8
  49.2 18.0 %collective-permute-done.1 = bf16[2,32,8,768]{3,1,2,0:T(8,128)(2,1)S(1)} collective-permute-done((bf16[2,32,8,768]{3,1,2,0:T(8,128)(2,1)S(1)}, bf16[2,32,8,768]{3,1,2,0:T(8,128)(2,1)S(1)}, u32[]{:S(2)}, u32[]{:S(2)}) %collective-permute-start.1) | collective-permute-done | bytes 786464 | tf_op jit(solution)/shard_map/ppermute | solution.py:8
  68.9 16.5 %collective-permute-done.2 = bf16[4,32,4,768]{3,1,2,0:T(8,128)(2,1)S(1)} collective-permute-done((bf16[4,32,4,768]{3,1,2,0:T(8,128)(2,1)S(1)}, bf16[4,32,4,768]{3,1,2,0:T(8,128)(2,1)S(1)}, u32[]{:S(2)}, u32[]{:S(2)}) %collective-permute-start.2) | collective-permute-done | bytes 786464 | tf_op jit(solution)/shard_map/ppermute | solution.py:8
  87.3 15.7 %collective-permute-done.3 = bf16[8,32,2,768]{3,1,2,0:T(8,128)(2,1)S(1)} collective-permute-done((bf16[8,32,2,768]{3,1,2,0:T(8,128)(2,1)S(1)}, bf16[8,32,2,768]{3,1,2,0:T(8,128)(2,1)S(1)}, u32[]{:S(2)}, u32[]{:S(2)}) %collective-permute-start.3) | collective-permute-done | bytes 786464 | tf_op jit(solution)/shard_map/ppermute | solution.py:8
  105.7 2.3 tile.10
  113.4 9.2 %while.10 = (s32[]{:T(128)}, bf16[2,512,768]{1,2,0:T(8,128)(2,1)}, s32[2]{0:T(128)S(1)}, bf16[1536,768]{1,0:T(8,128)(2,1)S(1)}, bf16[512,1024]{1,0:T(8,128)(2,1)S(1)}, /*index=5*/s32[]{:T(128)}, s32[]{:T(128)}, s32[]{:T(128)}) while((s32[]{:T(128)}, bf16[2,512,768]{1,2,0:T(8,128)(2,1)}, s32[2]{0:T(128)S(1)}, bf16[1536,768]{1,0:T(8,128)(2,1)S(1)}, ...), condition=%wide.region_2.3_spmd, body=%wide.region_1.2_spmd.sunk | while | flops 805306368 | bytes 4194951 | solution.py:75
  116.1 1.9 bitcast_dynamic-update-slice_fusion.2
  120.7 1.9 bitcast_dynamic-update-slice_fusion.2
  122.6 1.7 copy.173
  125.2 5.3 %collective-permute-start.5 = (bf16[1,1,16,24576]{3,2,1,0:T(8,128)(2,1)S(1)}, bf16[1,1,16,24576]{3,2,1,0:T(8,128)(2,1)S(1)}, u32[]{:S(2)}, u32[]{:S(2)}) collective-permute-start(bf16[1,1,16,24576]{3,2,1,0:T(8,128)(2,1)S(1)} %select_bitcast_fusion.5), channel_id=1, source_target_pairs={{0,16},{1,17},{2,18},{3,19},{4,20},{5,21},{6,22},{7,23},{8,24},{9,... | collective-permute-start | bytes 2359304 | tf_op jit(solution)/shard_map/ppermute | solution.py:8
  130.4 34.6 %collective-permute-done.5 = bf16[1,1,16,24576]{3,2,1,0:T(8,128)(2,1)S(1)} collective-permute-done((bf16[1,1,16,24576]{3,2,1,0:T(8,128)(2,1)S(1)}, bf16[1,1,16,24576]{3,2,1,0:T(8,128)(2,1)S(1)}, u32[]{:S(2)}, u32[]{:S(2)}) %collective-permute-start.5) | collective-permute-done | bytes 786464 | tf_op jit(solution)/shard_map/ppermute | solution.py:8
  165.8 18.4 %collective-permute-done.6 = bf16[2,1,8,24576]{3,2,0,1:T(8,128)(2,1)S(1)} collective-permute-done((bf16[2,1,8,24576]{3,2,0,1:T(8,128)(2,1)S(1)}, bf16[2,1,8,24576]{3,2,0,1:T(8,128)(2,1)S(1)}, u32[]{:S(2)}, u32[]{:S(2)}) %collective-permute-start.6) | collective-permute-done | bytes 786464 | tf_op jit(solution)/shard_map/ppermute | solution.py:8
  187.4 16.5 %collective-permute-done.7 = bf16[4,1,4,24576]{3,2,0,1:T(4,128)(2,1)S(1)} collective-permute-done((bf16[4,1,4,24576]{3,2,0,1:T(4,128)(2,1)S(1)}, bf16[4,1,4,24576]{3,2,0,1:T(4,128)(2,1)S(1)}, u32[]{:S(2)}, u32[]{:S(2)}) %collective-permute-start.7) | collective-permute-done | bytes 786464 | tf_op jit(solution)/shard_map/ppermute | solution.py:8
  205.8 1.6 copy.183
  209.8 15.7 %collective-permute-done.8 = bf16[8,1,2,24576]{3,0,2,1:T(8,128)(2,1)S(1)} collective-permute-done((bf16[8,1,2,24576]{3,0,2,1:T(8,128)(2,1)S(1)}, bf16[8,1,2,24576]{3,0,2,1:T(8,128)(2,1)S(1)}, u32[]{:S(2)}, u32[]{:S(2)}) %collective-permute-start.8) | collective-permute-done | bytes 786464 | tf_op jit(solution)/shard_map/ppermute | solution.py:8
  225.7 1.6 copy.184
  227.3 3.7 %broadcast_select_fusion = (bf16[16,1,1,1,24576]{4,2,0,3,1:T(2,128)(2,1)S(1)}, bf16[16,1,1,1,24576]{4,2,0,3,1:T(2,128)(2,1)S(1)}) fusion(pred[]{:T(512)S(6)} %eq.20, bf16[16,1,2,1,24576]{4,2,0,3,1:T(2,128)(2,1)S(1)} %bitcast.319), kind=kLoop, calls=%fused_computation.6 | loop fusion | flops 786432 | bytes 3145729 | tf_op jit(solution)/shard_map/jit(_where)/select_n | solution.py:29
  232.2 2.2 collective-permute-done.9
  239.1 2.3 reshape.698
  241.4 8.1 %fusion.5 = f32[32,4,3,2048]{3,0,2,1:T(8,128)S(1)} fusion(bf16[2048,2048]{1,0:T(8,128)(2,1)} %param.12, bf16[32,4,3,2048]{3,2,1,0:T(4,128)(2,1)} %reshape.698), kind=kOutput, calls=%fused_computation.4 | convolution fusion | flops 3221225472 | bytes 13107200 | tf_op jit(solution)/shard_map/dot_general | solution.py:79
  251.1 2.4 copy.188
  (87 shorter events, 30.2 us)
Async XLA Ops:
  9.2 38.5 %collective-permute-start = (bf16[1,32,16,768]{3,2,1,0:T(8,128)(2,1)S(1)}, bf16[1,32,16,768]{3,2,1,0:T(8,128)(2,1)S(1)}, u32[]{:S(2)}, u32[]{:S(2)}) collective-permute-start(bf16[1,32,16,768]{3,2,1,0:T(8,128)(2,1)S(1)} %fusion.28), channel_id=1, source_target_pairs={{0,16},{1,17},{2,18},{3,19},{4,20},{5,21},{6,22},{7,23},{8,24},{9,... | collective-permute-start | bytes 2359304 | tf_op jit(solution)/shard_map/ppermute | solution.py:8
  48.4 18.8 %collective-permute-start.1 = (bf16[2,32,8,768]{3,1,2,0:T(8,128)(2,1)S(1)}, bf16[2,32,8,768]{3,1,2,0:T(8,128)(2,1)S(1)}, u32[]{:S(2)}, u32[]{:S(2)}) collective-permute-start(bf16[2,32,8,768]{3,1,2,0:T(8,128)(2,1)S(1)} %select_bitcast_fusion.12), channel_id=1, source_target_pairs={{0,8},{1,9},{2,10},{3,11},{4,12},{5,13},{6,14},{7,15},{8,0},{9,1},... | collective-permute-start | bytes 2359304 | tf_op jit(solution)/shard_map/ppermute | solution.py:8
  67.5 17.9 %collective-permute-start.2 = (bf16[4,32,4,768]{3,1,2,0:T(8,128)(2,1)S(1)}, bf16[4,32,4,768]{3,1,2,0:T(8,128)(2,1)S(1)}, u32[]{:S(2)}, u32[]{:S(2)}) collective-permute-start(bf16[4,32,4,768]{3,1,2,0:T(8,128)(2,1)S(1)} %fusion.27), channel_id=1, source_target_pairs={{0,4},{1,5},{2,6},{3,7},{4,0},{5,1},{6,2},{7,3},{8,12},{9,13},{10,... | collective-permute-start | bytes 2359304 | tf_op jit(solution)/shard_map/ppermute | solution.py:8
  86.0 17.1 %collective-permute-start.3 = (bf16[8,32,2,768]{3,1,2,0:T(8,128)(2,1)S(1)}, bf16[8,32,2,768]{3,1,2,0:T(8,128)(2,1)S(1)}, u32[]{:S(2)}, u32[]{:S(2)}) collective-permute-start(bf16[8,32,2,768]{3,1,2,0:T(8,128)(2,1)S(1)} %fusion.26), channel_id=1, source_target_pairs={{0,2},{1,3},{2,0},{3,1},{4,6},{5,7},{6,4},{7,5},{8,10},{9,11},{10,... | collective-permute-start | bytes 2359304 | tf_op jit(solution)/shard_map/ppermute | solution.py:8
  103.5 0.7 copy-start.7
  103.6 6.9 %collective-permute-start.4 = (bf16[16,32,1,768]{3,1,0,2:T(8,128)(2,1)S(1)}, bf16[16,32,1,768]{3,1,0,2:T(8,128)(2,1)}, u32[]{:S(2)}, u32[]{:S(2)}) collective-permute-start(bf16[16,32,1,768]{3,1,0,2:T(8,128)(2,1)S(1)} %fusion.25), channel_id=1, source_target_pairs={{0,1},{1,0},{2,3},{3,2},{4,5},{5,4},{6,7},{7,6},{8,9},{9,8},{10,11... | collective-permute-start | bytes 2359304 | tf_op jit(solution)/shard_map/ppermute | solution.py:8
  108.0 1.2 slice-start
  112.2 1.2 copy-start.1
  125.2 39.8 %collective-permute-start.5 = (bf16[1,1,16,24576]{3,2,1,0:T(8,128)(2,1)S(1)}, bf16[1,1,16,24576]{3,2,1,0:T(8,128)(2,1)S(1)}, u32[]{:S(2)}, u32[]{:S(2)}) collective-permute-start(bf16[1,1,16,24576]{3,2,1,0:T(8,128)(2,1)S(1)} %select_bitcast_fusion.5), channel_id=1, source_target_pairs={{0,16},{1,17},{2,18},{3,19},{4,20},{5,21},{6,22},{7,23},{8,24},{9,... | collective-permute-start | bytes 2359304 | tf_op jit(solution)/shard_map/ppermute | solution.py:8
  165.3 18.9 %collective-permute-start.6 = (bf16[2,1,8,24576]{3,2,0,1:T(8,128)(2,1)S(1)}, bf16[2,1,8,24576]{3,2,0,1:T(8,128)(2,1)S(1)}, u32[]{:S(2)}, u32[]{:S(2)}) collective-permute-start(bf16[2,1,8,24576]{3,2,0,1:T(8,128)(2,1)S(1)} %fusion.24), channel_id=1, source_target_pairs={{0,8},{1,9},{2,10},{3,11},{4,12},{5,13},{6,14},{7,15},{8,0},{9,1},... | collective-permute-start | bytes 2359304 | tf_op jit(solution)/shard_map/ppermute | solution.py:8
  185.9 18.1 %collective-permute-start.7 = (bf16[4,1,4,24576]{3,2,0,1:T(4,128)(2,1)S(1)}, bf16[4,1,4,24576]{3,2,0,1:T(4,128)(2,1)S(1)}, u32[]{:S(2)}, u32[]{:S(2)}) collective-permute-start(bf16[4,1,4,24576]{3,2,0,1:T(4,128)(2,1)S(1)} %fusion.23), channel_id=1, source_target_pairs={{0,4},{1,5},{2,6},{3,7},{4,0},{5,1},{6,2},{7,3},{8,12},{9,13},{10,... | collective-permute-start | bytes 2359304 | tf_op jit(solution)/shard_map/ppermute | solution.py:8
  208.1 1.7 copy-start.5
  208.2 17.2 %collective-permute-start.8 = (bf16[8,1,2,24576]{3,0,2,1:T(8,128)(2,1)S(1)}, bf16[8,1,2,24576]{3,0,2,1:T(8,128)(2,1)S(1)}, u32[]{:S(2)}, u32[]{:S(2)}) collective-permute-start(bf16[8,1,2,24576]{3,0,2,1:T(8,128)(2,1)S(1)} %select_bitcast_fusion), channel_id=1, source_target_pairs={{0,2},{1,3},{2,0},{3,1},{4,6},{5,7},{6,4},{7,5},{8,10},{9,11},{10,... | collective-permute-start | bytes 2359304 | tf_op jit(solution)/shard_map/ppermute | solution.py:8
  231.1 1.0 copy-start.6
  231.1 1.0 copy-start.4
  232.0 2.4 collective-permute-start.9
  241.4 8.1 %copy-start.2 = (f32[32,3,2048]{2,0,1:T(8,128)S(1)}, f32[32,3,2048]{2,0,1:T(8,128)}, u32[]{:S(2)}) copy-start(f32[32,3,2048]{2,0,1:T(8,128)} %param.13) | copy-start | bytes 2359300
  249.5 0.7 copy-start.3
  250.0 0.9 copy-start
where the time goes:
time: 254 us; the launch traced here: 253 us
  waiting for transfers between devices  172 us (68%)
  local copies, waits for them, and re-layouts  34 us (13%)
  starting transfers between devices  16.6 us (7%)
  other arithmetic  13 us (5%)
  matrix products  12 us (5%)
  loops' own time  4.05 us (2%)
    ppermute x10, waiting for transfers between devices, from_partner(): lax.ppermute(value, axis, [(i, i ^ 1 << bit) for i in range(lax.axis_size...  172 us
    ppermute x10, starting transfers between devices, from_partner(): lax.ppermute(value, axis, [(i, i ^ 1 << bit) for i in range(lax.axis_size...  16.6 us
    unnamed x20, local copies, waits for them, and re-layouts  9.68 us
    dot_general x1, matrix products, body(): lax.dot_general(spanned, wall_filter, (((3,), (1,)), ((), ())), preferred...  8.12 us
    another operation x19, other arithmetic, butterfly(): jnp.stack([first, second], axis=1)  6.09 us
    another operation x3, local copies, waits for them, and re-layouts, butterfly(): halves = held.reshape(groups, inner_first, 2, targets // 2, inner_last)  5.62 us
    another operation x8, local copies, waits for them, and re-layouts, butterfly(): jnp.stack([first, second], axis=1)  5.58 us
  transfers between devices with their start and end apart: 10, of which 9 were waited for; matrix products, arithmetic and copies ran while one was open for 2% of the time, Pallas kernels for 0%

commit v1 on v0

--- a/solution.py
+++ b/solution.py
@@ -1,7 +1,252 @@
+import functools
+
 import jax
 import jax.numpy as jnp
 from jax import lax
+from jax.experimental import pallas as pl
+from jax.experimental.pallas import tpu as pltpu
 from jax.sharding import PartitionSpec as P
+
+LANES = 256
+MESH = pl.DeviceIdType.MESH
+
+
+def peer_of(step, me, count):
+    away = count // 2 + (1 - 2 * (step % 2)) * ((step + 1) // 2)
+    return lax.rem(me + away, count)
+
+
+def exchange_kernel(
+    count,
+    rows,
+    width,
+    pairs,
+    parts,
+    slim,
+    reach,
+    x_ref,
+    taps_ref,
+    wall_ref,
+    prev_ref,
+    scale_ref,
+    mean_ref,
+    diag_ref,
+    off_ref,
+    vel_ref,
+    state_ref,
+    wide,
+    summed,
+    back,
+    band,
+    wall,
+    decay,
+    inject,
+    wall_sem,
+    out_sem,
+    in_sem,
+    back_out_sem,
+    back_in_sem,
+):
+    me = lax.axis_index("span")
+    per = width // slim
+    group = pairs // parts
+    blocks = count * rows // reach
+
+    wall_copy = pltpu.make_async_copy(wall_ref, wall, wall_sem)
+    wall_copy.start()
+
+    barrier = pltpu.get_barrier_semaphore()
+
+    @pl.loop(0, count - 1)
+    def _(step):
+        pl.semaphore_signal(
+            barrier, inc=1, device_id=(peer_of(step, me, count),), device_id_type=MESH
+        )
+
+    pl.semaphore_wait(barrier, count - 1)
+
+    def columns(part, owner):
+        slot = part * count + owner
+        start = pl.multiple_of((slot % per) * slim, slim)
+        return slot // per, pl.ds(start, slim)
+
+    for part in range(parts):
+
+        @pl.loop(0, count - 1)
+        def _(step):
+            peer = peer_of(step, me, count)
+            pair, span = columns(part, peer)
+            pltpu.make_async_remote_copy(
+                src_ref=x_ref.at[pair, :, span],
+                dst_ref=wide.at[part, me],
+                send_sem=out_sem.at[part],
+                recv_sem=in_sem.at[part],
+                device_id=(peer,),
+                device_id_type=MESH,
+            ).start()
+
+        pair, span = columns(part, me)
+        pltpu.make_async_copy(x_ref.at[pair, :, span], wide.at[part, me], in_sem.at[part]).start()
+
+    weights = taps_ref[...]
+    taps = weights / jnp.sqrt(jnp.sum(weights * weights))
+    tall = jnp.broadcast_to(taps, (16, 3 * reach))
+    line = lax.broadcasted_iota(jnp.int32, (16, 3 * reach), 0)
+    for bit in range(4):
+        tall = jnp.where((line // (1 << bit)) % 2 == 1, pltpu.roll(tall, 1 << bit, 1), tall)
+
+    @pl.loop(0, reach // 16)
+    def _(step):
+        first = pl.multiple_of(step * 16, 16)
+        rolled = pltpu.roll(tall, first, 1)
+        band[pl.ds(first, 16), :] = rolled.astype(jnp.bfloat16)
+
+    decay[...] = jnp.exp(-jnp.pi / (2.0 * scale_ref[...]))
+    inject[...] = jnp.sqrt(1.0 - jnp.exp(-jnp.pi / scale_ref[...]))
+    state_ref[...] = prev_ref[...]
+
+    for part in range(parts):
+        pltpu.make_async_copy(wide.at[part], wide.at[part], in_sem.at[part]).wait()
+        share = reach // rows
+        for block in range(blocks):
+            total = jnp.zeros((reach, slim), jnp.float32)
+            for shift in range(3):
+                source = (block - 1 + shift) % blocks
+                chunk = wide[part, source * share : (source + 1) * share].reshape(reach, slim)
+                total += jnp.dot(
+                    band[:, shift * reach : (shift + 1) * reach],
+                    chunk,
+                    preferred_element_type=jnp.float32,
+                )
+            summed[part, block * share : (block + 1) * share] = total.astype(
+                jnp.bfloat16
+            ).reshape(share, rows, slim)
+
+        pair, span = columns(part, me)
+
+        @pl.loop(0, count - 1)
+        def _(step):
+            peer = peer_of(step, me, count)
+            pltpu.make_async_remote_copy(
+                src_ref=summed.at[part, peer],
+                dst_ref=back.at[pair, :, span],
+                send_sem=back_out_sem.at[part],
+                recv_sem=back_in_sem.at[part],
+                device_id=(peer,),
+                device_id_type=MESH,
+            ).start()
+
+        pltpu.make_async_copy(
+            summed.at[part, me], back.at[pair, :, span], back_in_sem.at[part]
+        ).start()
+
+    wall_copy.wait()
+    tile = min(256, width)
+    for part in range(parts):
+        mine = back.at[part * group : (part + 1) * group]
+        pltpu.make_async_copy(mine, mine, back_in_sem.at[part]).wait()
+
+        @pl.loop(0, width // tile)
+        def _(step):
+            at = pl.ds(pl.multiple_of(step * tile, tile), tile)
+            filtered = lax.dot_general(
+                back[part * group : (part + 1) * group].reshape(group * rows, width),
+                wall[at, :],
+                (((1,), (1,)), ((), ())),
+                preferred_element_type=jnp.float32,
+            ).reshape(group, rows, tile)
+            for local in range(group):
+                pair = part * group + local
+                component = pair % 3
+                one = pl.ds(component, 1)
+                new = decay[one, at] * state_ref[component, :, at] + inject[one, at] * filtered[local]
+                state_ref[component, :, at] = new
+                if component == 0:
+                    value = mean_ref[:, at] + diag_ref[0:1, at] * new
+                elif component == 1:
+                    value = off_ref[0:1, at] * state_ref[0, :, at] + diag_ref[1:2, at] * new
+                else:
+                    value = (
+                        off_ref[1:2, at] * state_ref[0, :, at]
+                        + off_ref[2:3, at] * state_ref[1, :, at]
+                        + diag_ref[2:3, at] * new
+                    )
+                vel_ref[pair, :, at] = value.astype(jnp.bfloat16)
+
+    for part in range(parts):
+        sent = wide.at[part, 0 : count - 1]
+        pltpu.make_async_copy(sent, sent, out_sem.at[part]).wait()
+        pltpu.make_async_copy(sent, sent, back_out_sem.at[part]).wait()
+
+
+def fits(count, rows, pairs, width, reach, slim):
+    columns = pairs * width
+    return (
+        columns % (count * slim) == 0
+        and (count * slim) % width == 0
+        and width % slim == 0
+        and rows % 16 == 0
+        and reach % rows == 0
+        and reach % 128 == 0
+        and count * rows % reach == 0
+        and count * rows // reach >= 3
+    )
+
+
+def exchanged(
+    random_slabs,
+    span_weights,
+    wall_filter,
+    prev_state,
+    time_scale,
+    mean_velocity,
+    lund_diag,
+    lund_off,
+):
+    count = lax.axis_size("span")
+    rows, planes, kinds, width = random_slabs.shape
+    pairs = planes * kinds
+    reach = (span_weights.shape[0] - 1) // 2
+    slim = LANES
+    parts = pairs * width // (count * slim)
+    x = random_slabs.transpose(1, 2, 0, 3).reshape(pairs, rows, width)
+    padded = jnp.pad(span_weights, (0, 3 * reach - span_weights.shape[0])).reshape(1, 3 * reach)
+    in_vmem = pl.BlockSpec(memory_space=pltpu.VMEM)
+    velocity, state = pl.pallas_call(
+        functools.partial(exchange_kernel, count, rows, width, pairs, parts, slim, reach),
+        out_shape=(
+            jax.ShapeDtypeStruct((pairs, rows, width), jnp.bfloat16),
+            jax.ShapeDtypeStruct((kinds, rows, width), jnp.float32),
+        ),
+        in_specs=[in_vmem, in_vmem, pl.BlockSpec(memory_space=pl.ANY)] + [in_vmem] * 5,
+        out_specs=(in_vmem, in_vmem),
+        scratch_shapes=[
+            pltpu.VMEM((parts, count, rows, slim), jnp.bfloat16),
+            pltpu.VMEM((parts, count, rows, slim), jnp.bfloat16),
+            pltpu.VMEM((pairs, rows, width), jnp.bfloat16),
+            pltpu.VMEM((reach, 3 * reach), jnp.bfloat16),
+            pltpu.VMEM((width, width), jnp.bfloat16),
+            pltpu.VMEM((kinds, width), jnp.float32),
+            pltpu.VMEM((kinds, width), jnp.float32),
+            pltpu.SemaphoreType.DMA,
+            pltpu.SemaphoreType.DMA((parts,)),
+            pltpu.SemaphoreType.DMA((parts,)),
+            pltpu.SemaphoreType.DMA((parts,)),
+            pltpu.SemaphoreType.DMA((parts,)),
+        ],
+        compiler_params=pltpu.CompilerParams(collective_id=0, has_side_effects=True),
+    )(
+        x,
+        padded,
+        wall_filter,
+        prev_state.transpose(1, 0, 2),
+        time_scale,
+        mean_velocity.reshape(1, width),
+        lund_diag,
+        lund_off,
+    )
+    velocity = velocity.reshape(planes, kinds, rows, width).transpose(2, 0, 1, 3)
+    return velocity, state.transpose(1, 0, 2)
 
 
 def from_partner(value, axis, bit):
@@ -54,6 +299,18 @@
     planes = random_slabs.shape[1]
     width = random_slabs.shape[3]
     columns = planes * 3 * width
+    half = (span_weights.shape[0] - 1) // 2
+    if fits(lax.axis_size("span"), rows, planes * 3, width, half, LANES):
+        return exchanged(
+            random_slabs,
+            span_weights,
+            wall_filter,
+            prev_state,
+            time_scale,
+            mean_velocity,
+            lund_diag,
+            lund_off,
+        )
     flat = random_slabs.reshape(rows, columns)
     scaling = jnp.sqrt(jnp.sum(span_weights * span_weights))
     taps = (span_weights / scaling).astype(jnp.bfloat16)

time: 254 us -> 92.7 us (0.36)
  waiting for transfers between devices: 172 us -> 0 us
  Pallas kernels: 0 us -> 82.4 us
  local copies, waits for them, and re-layouts: 34 us -> 9.41 us
  starting transfers between devices: 16.6 us -> 0 us
  other arithmetic: 13 us -> 0 us
  matrix products: 12 us -> 0 us
  loops' own time: 4.05 us -> 0 us
    ppermute x10 -> x0, waiting for transfers between devices: 172 us -> none  [from_partner(): lax.ppermute(value, axis, [(i, i ^ 1 << bit) for i in range(lax.axis_size...]
    pallas_call x0 -> x1, Pallas kernels: none -> 82.4 us  [exchanged(): pl.pallas_call(functools.partial(exchange_kernel, count, rows, width, pai...]
    ppermute x10 -> x0, starting transfers between devices: 16.6 us -> none  [from_partner(): lax.ppermute(value, axis, [(i, i ^ 1 << bit) for i in range(lax.axis_size...]
    another operation x14 -> x0, local copies, waits for them, and re-layouts: 14.8 us -> none  [the longest x3 5.62 us: butterfly(): halves = held.reshape(groups, inner_first, 2, targets // 2, inner_last)]
    dot_general x3 -> x0, matrix products: 12 us -> none  [the longest x1 8.12 us: body(): lax.dot_general(spanned, wall_filter, (((3,), (1,)), ((), ())), preferred...]
    unnamed x20 -> x3, local copies, waits for them, and re-layouts: 9.68 us -> 0.88 us
    another operation x22 -> x0, other arithmetic: 6.79 us -> none  [the longest x19 6.09 us: butterfly(): jnp.stack([first, second], axis=1)]
    select_n x10 -> x0, other arithmetic: 4.85 us -> none  [the longest x1 3.71 us: butterfly(): kept = jnp.where(upper, higher, lower)]
  transfers between devices with their start and end apart: 10 -> 0, of which waited for: 9 -> 0; matrix products, arithmetic and copies ran while one was open for 2% -> 0% of each run, Pallas kernels for 0% -> 0%
where the time goes in v1:
time: 92.7 us; the launch traced here: 92.5 us
  Pallas kernels  82.4 us (89%)
  local copies, waits for them, and re-layouts  9.41 us (10%)
    pallas_call x1, Pallas kernels, exchanged(): pl.pallas_call(functools.partial(exchange_kernel, count, rows, width, pai...  82.4 us
    reshape x1, local copies, waits for them, and re-layouts, exchanged(): velocity.reshape(planes, kinds, rows, width).transpose(2, 0, 1, 3)  3.84 us
    transpose x1, local copies, waits for them, and re-layouts, exchanged(): x = random_slabs.transpose(1, 2, 0, 3).reshape(pairs, rows, width)  3.41 us

profile of v1, /device:TPU:0, one launch (start us, length us, event | category | flops | bytes accessed | tf_op | source)
XLA Modules:
  0.0 92.5 jit_solution(15629651203718026762)
XLA Ops:
  0.6 0.7 pad.4
  1.3 0.6 reshape.17.taps_ref
  1.9 3.4 %copy.10 = bf16[4,3,32,2048]{3,2,1,0:T(8,128)(2,1)} copy(bf16[4,3,32,2048]{3,0,1,2:T(4,128)(2,1)} %bitcast.10) | data formatting | bytes 3145728 | tf_op jit(solution)/shard_map/transpose | solution.py:212
  5.3 82.4 %shard_map.95 = (bf16[12,32,2048]{2,1,0:T(8,128)(2,1)}, f32[3,32,2048]{2,1,0:T(8,128)}) custom-call(bf16[12,32,2048]{2,1,0:T(8,128)(2,1)} %bitcast.9, f32[1,768]{1,0:T(1,128)} %reshape.17.taps_ref, bf16[2048,2048]{1,0:T(8,128)(2,1)} %wall_ref.1, f32[3,32,2048]{2,1,0:T(8,128)} %bitcast.14, f32[3,2048]{1,0:T(4,128)} %scale_ref.1, f32[1,2048]{1,0:T(1,128)} %bitcast.15, ...), custom_call_target="tpu_custom_call" | custom-call | tf_op jit(solution)/shard_map/pallas_call | solution.py:215
  87.7 0.0 copy-start
  87.7 3.8 %copy.13 = bf16[4,3,32,2048]{3,0,1,2:T(4,128)(2,1)} copy(bf16[4,3,32,2048]{3,2,1,0:T(8,128)(2,1)} %bitcast.12) | data formatting | bytes 3145728 | tf_op jit(solution)/shard_map/reshape | solution.py:248
  91.6 0.0 copy-done
  91.6 0.9 copy.15
Async XLA Ops:
  87.7 3.9 %copy-start = (f32[3,32,2048]{2,1,0:T(8,128)S(1)}, f32[3,32,2048]{2,1,0:T(8,128)}, u32[]{:S(2)}) copy-start(f32[3,32,2048]{2,1,0:T(8,128)} %get-tuple-element.5) | copy-start | bytes 2359300

commit v2 on v1

--- a/solution.py
+++ b/solution.py
@@ -24,7 +24,7 @@
     parts,
     slim,
     reach,
-    x_ref,
+    slab_ref,
     taps_ref,
     wall_ref,
     prev_ref,
@@ -34,11 +34,13 @@
     off_ref,
     vel_ref,
     state_ref,
+    x_ref,
     wide,
     summed,
     back,
     band,
     wall,
+    early,
     decay,
     inject,
     wall_sem,
@@ -63,14 +65,25 @@
             barrier, inc=1, device_id=(peer_of(step, me, count),), device_id_type=MESH
         )
 
+    def relayout(part):
+        for pair in range(part * group, (part + 1) * group):
+            x_ref[pair] = slab_ref[:, pair % 3, pair // 3, :]
+
+    relayout(0)
     pl.semaphore_wait(barrier, count - 1)
 
+    half = count // 2
+    side = per // 2
+    ours = me // half
+
     def columns(part, owner):
-        slot = part * count + owner
-        start = pl.multiple_of((slot % per) * slim, slim)
-        return slot // per, pl.ds(start, slim)
+        place = owner % half
+        start = pl.multiple_of((owner // half * side + place % side) * slim, slim)
+        return part * group + place // side, pl.ds(start, slim)
 
     for part in range(parts):
+        if part:
+            relayout(part)
 
         @pl.loop(0, count - 1)
         def _(step):
@@ -88,7 +101,9 @@
         pair, span = columns(part, me)
         pltpu.make_async_copy(x_ref.at[pair, :, span], wide.at[part, me], in_sem.at[part]).start()
 
-    weights = taps_ref[...]
+    weights = jnp.concatenate(
+        [taps_ref[...], jnp.zeros((3 * reach - taps_ref.shape[0],), jnp.float32)]
+    ).reshape(1, 3 * reach)
     taps = weights / jnp.sqrt(jnp.sum(weights * weights))
     tall = jnp.broadcast_to(taps, (16, 3 * reach))
     line = lax.broadcasted_iota(jnp.int32, (16, 3 * reach), 0)
@@ -131,47 +146,62 @@
                 src_ref=summed.at[part, peer],
                 dst_ref=back.at[pair, :, span],
                 send_sem=back_out_sem.at[part],
-                recv_sem=back_in_sem.at[part],
+                recv_sem=back_in_sem.at[part, (peer // half + ours) % 2],
                 device_id=(peer,),
                 device_id_type=MESH,
             ).start()
 
         pltpu.make_async_copy(
-            summed.at[part, me], back.at[pair, :, span], back_in_sem.at[part]
+            summed.at[part, me], back.at[pair, :, span], back_in_sem.at[part, 0]
         ).start()
+
+    def finish(part, at, filtered):
+        for local in range(group):
+            pair = part * group + local
+            component = pair % 3
+            one = pl.ds(component, 1)
+            new = decay[one, at] * state_ref[component, :, at] + inject[one, at] * filtered[local]
+            state_ref[component, :, at] = new
+            if component == 0:
+                value = mean_ref[:, at] + diag_ref[0:1, at] * new
+            elif component == 1:
+                value = off_ref[0:1, at] * state_ref[0, :, at] + diag_ref[1:2, at] * new
+            else:
+                value = (
+                    off_ref[1:2, at] * state_ref[0, :, at]
+                    + off_ref[2:3, at] * state_ref[1, :, at]
+                    + diag_ref[2:3, at] * new
+                )
+            vel_ref[pair, :, at] = value.astype(jnp.bfloat16)
 
     wall_copy.wait()
     tile = min(256, width)
     for part in range(parts):
-        mine = back.at[part * group : (part + 1) * group]
-        pltpu.make_async_copy(mine, mine, back_in_sem.at[part]).wait()
-
-        @pl.loop(0, width // tile)
-        def _(step):
-            at = pl.ds(pl.multiple_of(step * tile, tile), tile)
-            filtered = lax.dot_general(
-                back[part * group : (part + 1) * group].reshape(group * rows, width),
-                wall[at, :],
-                (((1,), (1,)), ((), ())),
-                preferred_element_type=jnp.float32,
-            ).reshape(group, rows, tile)
-            for local in range(group):
-                pair = part * group + local
-                component = pair % 3
-                one = pl.ds(component, 1)
-                new = decay[one, at] * state_ref[component, :, at] + inject[one, at] * filtered[local]
-                state_ref[component, :, at] = new
-                if component == 0:
-                    value = mean_ref[:, at] + diag_ref[0:1, at] * new
-                elif component == 1:
-                    value = off_ref[0:1, at] * state_ref[0, :, at] + diag_ref[1:2, at] * new
+        held = back.at[part * group : (part + 1) * group]
+        for far in range(2):
+            first = pl.multiple_of((ours + far) % 2 * (width // 2), width // 2)
+            span = pl.ds(first, width // 2)
+            mine = held.at[:, :, 0 : width // 2]
+            pltpu.make_async_copy(mine, mine, back_in_sem.at[part, far]).wait()
+            if part < parts - 1 and far == 0:
+                continue
+
+            @pl.loop(0, width // tile)
+            def _(step):
+                at = pl.ds(pl.multiple_of(step * tile, tile), tile)
+                reading = span if part == parts - 1 else slice(None)
+                filtered = lax.dot_general(
+                    held[:, :, reading].reshape(group * rows, -1),
+                    wall[at, reading],
+                    (((1,), (1,)), ((), ())),
+                    preferred_element_type=jnp.float32,
+                ).reshape(group, rows, tile)
+                if far == 0:
+                    early[:, :, at] = filtered
                 else:
-                    value = (
-                        off_ref[1:2, at] * state_ref[0, :, at]
-                        + off_ref[2:3, at] * state_ref[1, :, at]
-                        + diag_ref[2:3, at] * new
-                    )
-                vel_ref[pair, :, at] = value.astype(jnp.bfloat16)
+                    if part == parts - 1:
+                        filtered += early[:, :, at]
+                    finish(part, at, filtered)
 
     for part in range(parts):
         sent = wide.at[part, 0 : count - 1]
@@ -184,7 +214,8 @@
     return (
         columns % (count * slim) == 0
         and (count * slim) % width == 0
-        and width % slim == 0
+        and width % (2 * slim) == 0
+        and count % 2 == 0
         and rows % 16 == 0
         and reach % rows == 0
         and reach % 128 == 0
@@ -209,8 +240,7 @@
     reach = (span_weights.shape[0] - 1) // 2
     slim = LANES
     parts = pairs * width // (count * slim)
-    x = random_slabs.transpose(1, 2, 0, 3).reshape(pairs, rows, width)
-    padded = jnp.pad(span_weights, (0, 3 * reach - span_weights.shape[0])).reshape(1, 3 * reach)
+    x = random_slabs.transpose(0, 2, 1, 3)
     in_vmem = pl.BlockSpec(memory_space=pltpu.VMEM)
     velocity, state = pl.pallas_call(
         functools.partial(exchange_kernel, count, rows, width, pairs, parts, slim, reach),
@@ -221,23 +251,25 @@
         in_specs=[in_vmem, in_vmem, pl.BlockSpec(memory_space=pl.ANY)] + [in_vmem] * 5,
         out_specs=(in_vmem, in_vmem),
         scratch_shapes=[
+            pltpu.VMEM((pairs, rows, width), jnp.bfloat16),
             pltpu.VMEM((parts, count, rows, slim), jnp.bfloat16),
             pltpu.VMEM((parts, count, rows, slim), jnp.bfloat16),
             pltpu.VMEM((pairs, rows, width), jnp.bfloat16),
             pltpu.VMEM((reach, 3 * reach), jnp.bfloat16),
             pltpu.VMEM((width, width), jnp.bfloat16),
+            pltpu.VMEM((pairs // parts, rows, width), jnp.float32),
             pltpu.VMEM((kinds, width), jnp.float32),
             pltpu.VMEM((kinds, width), jnp.float32),
             pltpu.SemaphoreType.DMA,
             pltpu.SemaphoreType.DMA((parts,)),
             pltpu.SemaphoreType.DMA((parts,)),
             pltpu.SemaphoreType.DMA((parts,)),
-            pltpu.SemaphoreType.DMA((parts,)),
+            pltpu.SemaphoreType.DMA((parts, 2)),
         ],
         compiler_params=pltpu.CompilerParams(collective_id=0, has_side_effects=True),
     )(
         x,
-        padded,
+        span_weights,
         wall_filter,
         prev_state.transpose(1, 0, 2),
         time_scale,

time: 92.7 us -> 87.3 us (0.942)
  local copies, waits for them, and re-layouts: 9.41 us -> 4.72 us
    transpose x1 -> x0, local copies, waits for them, and re-layouts: 3.41 us -> none  [exchanged(): x = random_slabs.transpose(1, 2, 0, 3).reshape(pairs, rows, width)]
where the time goes in v2:
time: 87.3 us; the launch traced here: 87.1 us
  Pallas kernels  81.7 us (94%)
  local copies, waits for them, and re-layouts  4.72 us (5%)
    pallas_call x1, Pallas kernels, exchanged(): pl.pallas_call(functools.partial(exchange_kernel, count, rows, width, pai...  81.7 us
    reshape x1, local copies, waits for them, and re-layouts, exchanged(): velocity.reshape(planes, kinds, rows, width).transpose(2, 0, 1, 3)  3.84 us

profile of v2, /device:TPU:0, one launch (start us, length us, event | category | flops | bytes accessed | tf_op | source)
XLA Modules:
  0.0 87.1 jit_solution(15482065532467604961)
XLA Ops:
  0.6 81.7 %shard_map.95 = (bf16[12,32,2048]{2,1,0:T(8,128)(2,1)}, f32[3,32,2048]{2,1,0:T(8,128)}) custom-call(bf16[32,3,4,2048]{3,2,1,0:T(4,128)(2,1)} %bitcast.10, f32[513]{0:T(1024)} %taps_ref.1, bf16[2048,2048]{1,0:T(8,128)(2,1)} %wall_ref.1, f32[3,32,2048]{2,1,0:T(8,128)} %bitcast.11, f32[3,2048]{1,0:T(4,128)} %scale_ref.1, f32[1,2048]{1,0:T(1,128)} %bitcast.13, ...), custom_call_target="tpu_custom_call" | custom-call | tf_op jit(solution)/shard_map/pallas_call | solution.py:245
  82.4 0.0 copy-start
  82.4 3.8 %copy.12 = bf16[4,3,32,2048]{3,0,1,2:T(4,128)(2,1)} copy(bf16[4,3,32,2048]{3,2,1,0:T(8,128)(2,1)} %bitcast.9) | data formatting | bytes 3145728 | tf_op jit(solution)/shard_map/reshape | solution.py:280
  86.2 0.0 copy-done
  86.2 0.9 %copy.14 = f32[32,3,2048]{2,0,1:T(8,128)} copy(f32[32,3,2048]{2,0,1:T(8,128)S(1)} %bitcast.12) | data formatting | bytes 1572864
Async XLA Ops:
  82.4 3.9 %copy-start = (f32[3,32,2048]{2,1,0:T(8,128)S(1)}, f32[3,32,2048]{2,1,0:T(8,128)}, u32[]{:S(2)}) copy-start(f32[3,32,2048]{2,1,0:T(8,128)} %get-tuple-element.5) | copy-start | bytes 2359300

commit v3 on v2

--- a/solution.py
+++ b/solution.py
@@ -248,7 +248,7 @@
             jax.ShapeDtypeStruct((pairs, rows, width), jnp.bfloat16),
             jax.ShapeDtypeStruct((kinds, rows, width), jnp.float32),
         ),
-        in_specs=[in_vmem, in_vmem, pl.BlockSpec(memory_space=pl.ANY)] + [in_vmem] * 5,
+        in_specs=[in_vmem, in_vmem, pl.BlockSpec(memory_space=pltpu.HBM)] + [in_vmem] * 5,
         out_specs=(in_vmem, in_vmem),
         scratch_shapes=[
             pltpu.VMEM((pairs, rows, width), jnp.bfloat16),
@@ -266,7 +266,7 @@
             pltpu.SemaphoreType.DMA((parts,)),
             pltpu.SemaphoreType.DMA((parts, 2)),
         ],
-        compiler_params=pltpu.CompilerParams(collective_id=0, has_side_effects=True),
+        compiler_params=pltpu.CompilerParams(collective_id=0, has_side_effects=True, vmem_limit_bytes=48 * 2**20),
     )(
         x,
         span_weights,

time: 87.3 us -> 89.2 us (1.022)
  local copies, waits for them, and re-layouts: 4.72 us -> 9.43 us
  Pallas kernels: 81.7 us -> 78.6 us
    unnamed x3 -> x15, local copies, waits for them, and re-layouts: 0.88 us -> 7.07 us
    pallas_call x1, Pallas kernels: 81.7 us -> 78.6 us  [exchanged(): pl.pallas_call(functools.partial(exchange_kernel, count, rows, width, pai...]
    reshape x1, local copies, waits for them, and re-layouts: 3.84 us -> 2.36 us  [exchanged(): velocity.reshape(planes, kinds, rows, width).transpose(2, 0, 1, 3)]
where the time goes in v3:
time: 89.2 us; the launch traced here: 88.7 us
  Pallas kernels  78.6 us (88%)
  local copies, waits for them, and re-layouts  9.43 us (11%)
    pallas_call x1, Pallas kernels, exchanged(): pl.pallas_call(functools.partial(exchange_kernel, count, rows, width, pai...  78.6 us
    unnamed x15, local copies, waits for them, and re-layouts  7.07 us
    reshape x1, local copies, waits for them, and re-layouts, exchanged(): velocity.reshape(planes, kinds, rows, width).transpose(2, 0, 1, 3)  2.36 us

profile of v3, /device:TPU:0, one launch (start us, length us, event | category | flops | bytes accessed | tf_op | source)
XLA Modules:
  0.0 88.7 jit_solution(16252068514335912835)
XLA Ops:
  0.6 0.0 copy-start
  0.6 1.4 %copy-done = bf16[32,4,3,2048]{3,1,2,0:T(4,128)(2,1)S(1)} copy-done((bf16[32,4,3,2048]{3,1,2,0:T(4,128)(2,1)S(1)}, bf16[32,4,3,2048]{3,1,2,0:T(4,128)(2,1)}, u32[]{:S(2)}) %copy-start) | copy-done | bytes 1572888
  2.0 0.0 copy-start.1
  2.0 1.1 %copy-done.1 = f32[32,3,2048]{2,0,1:T(8,128)S(1)} copy-done((f32[32,3,2048]{2,0,1:T(8,128)S(1)}, f32[32,3,2048]{2,0,1:T(8,128)}, u32[]{:S(2)}) %copy-start.1) | copy-done | bytes 786456
  3.2 0.0 copy-start.2
  3.2 0.8 copy-done.2
  3.9 0.0 copy-start.3
  3.9 0.8 copy-done.3
  4.7 0.0 copy-start.4
  4.7 0.8 copy-done.4
  5.5 0.0 copy-start.5
  5.5 0.7 copy-done.5
  6.1 0.0 copy-start.6
  6.2 0.7 copy-done.6
  6.8 78.6 %shard_map.95 = (bf16[12,32,2048]{2,1,0:T(8,128)(2,1)S(1)}, f32[3,32,2048]{2,1,0:T(8,128)S(1)}) custom-call(bf16[32,3,4,2048]{3,2,1,0:T(4,128)(2,1)S(1)} %bitcast.9, f32[513]{0:T(1024)S(1)} %copy-done.6, bf16[2048,2048]{1,0:T(8,128)(2,1)} %wall_ref.1, f32[3,32,2048]{2,1,0:T(8,128)S(1)} %bitcast.10, f32[3,2048]{1,0:T(4,128)S(1)} %copy-done.2, ...), custom_call_target="tpu_custom_call" | custom-call | tf_op jit(solution)/shard_map/pallas_call | solution.py:245
  85.5 2.4 %copy.12 = bf16[4,3,32,2048]{3,0,1,2:T(4,128)(2,1)} copy(bf16[4,3,32,2048]{3,2,1,0:T(8,128)(2,1)S(1)} %bitcast.8) | data formatting | bytes 3145728 | tf_op jit(solution)/shard_map/reshape | solution.py:280
  87.8 0.9 copy.14
Async XLA Ops:
  0.6 1.4 %copy-start = (bf16[32,4,3,2048]{3,1,2,0:T(4,128)(2,1)S(1)}, bf16[32,4,3,2048]{3,1,2,0:T(4,128)(2,1)}, u32[]{:S(2)}) copy-start(bf16[32,4,3,2048]{3,1,2,0:T(4,128)(2,1)} %param.8) | copy-start | bytes 4718596
  2.0 1.1 %copy-start.1 = (f32[32,3,2048]{2,0,1:T(8,128)S(1)}, f32[32,3,2048]{2,0,1:T(8,128)}, u32[]{:S(2)}) copy-start(f32[32,3,2048]{2,0,1:T(8,128)} %param.11) | copy-start | bytes 2359300
  3.2 0.8 copy-start.2
  3.9 0.8 copy-start.3
  4.7 0.8 copy-start.4
  5.5 0.7 copy-start.5
  6.1 0.7 copy-start.6
